TPU v7x, 32 devices: a whole 2x2x4 slice. The times are simulated.
32 devices in a mesh: col: 16 (over z, y, x), lev: 2 (over core).
Axes of the slice: x: 2, y: 2, z: 4, core: 2. Of those that a mesh axis runs over, the one named last changes fastest.
Arguments:
- perturbations: float32 [80, 16, 16384], P(None, 'lev', 'col'), may hold values from -0.625 to 0.625
- gradient: float32 [32, 16, 16384], P(None, 'lev', 'col'), may hold values from -2 to 2
- horizontal: float32 [20, 16384], P(None, 'col'), may hold values from -50 to 50
- area: float32 [16384], P('col'), may hold values from 1 to 60
- vertical: float32 [20, 16], P(None, 'lev'), may hold values from -1.25 to 1.25
Outputs:
- increment: float32 [32, 16, 16384], P(None, 'lev', 'col')
- background: float32 [32], replicated
All inputs are finite; a program needn't handle non-finite values.
Results may differ from a plain program's by a relative error of at most 0.0003.
Values sent between devices are 32-bit elements; how exact they have to be, the bound alone decides.
A program may use at most 128 MiB of HBM per device.

v0:
```python
import jax
import jax.numpy as jnp
from jax import lax
from jax.sharding import PartitionSpec as P

TOP_PRECISION = lax.Precision.HIGHEST


def adjoint_terms(perturbations, weighted, modes):
    mode_products = weighted[:, :, None, :] * modes[None, None, :, :]
    return jnp.einsum("klc,vlbc->lkvb", perturbations, mode_products, precision=TOP_PRECISION)


def project_levels(vertical, terms):
    return jnp.einsum("al,lkvb->vkab", vertical, terms, precision=TOP_PRECISION)


def mode_factor(mode_power, area_sum, count_modes):
    return 1.0 / jnp.sqrt(count_modes * (mode_power / area_sum + 1e-06))


def per_device(perturbations, gradient, horizontal, area, vertical):
    count_modes = horizontal.shape[0]
    columns = horizontal.shape[1] * lax.axis_size("col")
    power_local = jnp.sum(area[None, :] * horizontal * horizontal, axis=1)
    area_local = jnp.sum(area)
    weighted = gradient * (area * columns)[None, None, :]
    terms = adjoint_terms(perturbations, weighted, horizontal)
    summed, doubled_power, doubled = lax.psum(
        (project_levels(vertical, terms), power_local, area_local), ("col", "lev")
    )
    area_sum = doubled / lax.axis_size("lev")
    mode_power = doubled_power / lax.axis_size("lev")
    factor = mode_factor(mode_power, area_sum, count_modes)
    scaled_terms = horizontal * factor[:, None]
    control = summed * (factor / area_sum)[None, None, None, :]
    lifted = jnp.einsum("al,vkab->lkvb", vertical, control, precision=TOP_PRECISION)
    member_spread = jnp.einsum("lkvb,klc->lvbc", lifted, perturbations, precision=TOP_PRECISION)
    increment = jnp.einsum("trxa,xa->rta", member_spread, scaled_terms, precision=TOP_PRECISION)
    background = 0.5 * jnp.sum(control * control, axis=(1, 2, 3))
    return (increment, background)


def solution(mesh):
    return jax.shard_map(
        per_device,
        mesh=mesh,
        in_specs=(
            P(None, "lev", "col"),
            P(None, "lev", "col"),
            P(None, "col"),
            P("col"),
            P(None, "lev"),
        ),
        out_specs=(P(None, "lev", "col"), P()),
        check_vma=False,
    )
```

profile of v0, /device:TPU:0, one launch (start us, length us, event | category | flops | bytes accessed | tf_op | source)
XLA Modules:
  0.0 289.0 jit_solution(13503806161520612798)
XLA Ops:
  7.2 0.0 copy-start
  7.2 0.0 all-reduce.3.cloned.1.call-start
  7.2 1.4 broadcast_multiply_fusion.2
  8.7 1.3 broadcast_multiply_fusion.1
  10.0 10.6 %broadcast_multiply_fusion = f32[32,8,20,1024]{3,1,2,0:T(8,128)} fusion(f32[20,1024]{1,0:T(8,128)} %param.7, f32[32,8,1024]{2,1,0:T(8,128)S(1)} %broadcast_multiply_fusion.1), kind=kLoop, calls=%fused_computation.3 | loop fusion | flops 5242880 | bytes 22102016 | tf_op jit(solution)/shard_map/mul | solution.py:10
  20.6 0.0 copy-done
  20.6 0.0 copy-start.2
  20.6 38.6 %fusion.12 = f32[8,80,32,20]{1,2,3,0:T(8,128)S(1)} fusion(f32[80,8,1024,1]{2,1,0,3:T(8,128)S(1)} %bitcast.23, f32[32,8,20,1024]{3,1,2,0:T(8,128)} %broadcast_multiply_fusion), kind=kOutput, calls=%fused_computation.14 | convolution fusion | flops 5033164800 | bytes 25231360 | tf_op jit(solution)/shard_map/klc,vlbc->lkvb/dot_general | solution.py:11
  59.2 0.0 copy-done.2
  59.2 0.0 copy-start.1
  59.2 0.0 copy-start.3
  59.2 10.3 %convolution_bitcast_fusion = f32[32,80,20,20]{1,2,3,0:T(8,128)} fusion(f32[8,80,32,20]{1,2,3,0:T(8,128)S(1)} %fusion.12, f32[20,8]{0,1:T(8,128)S(1)} %copy-done.2), kind=kOutput, calls=%fused_computation.9 | convolution fusion | flops 98304000 | bytes 5735040 | tf_op jit(solution)/shard_map/al,lkvb->vkab/dot_general | solution.py:15
  69.5 0.0 all-reduce.3.cloned.1.call-update
  69.6 0.0 copy-done.1
  69.6 0.0 copy-done.3
  69.6 0.1 fusion.17
  69.7 43.9 %all-reduce = (f32[20]{0:T(128)S(1)}, f32[]{:T(128)}) all-reduce(f32[20]{0:T(128)S(1)} %fusion.17, f32[]{:T(128)} %get-tuple-element.7), channel_id=1, replica_groups=mesh['col'=16,'lev'=2] {'col','lev'}, use_global_device_ids=true, to_apply=%region_1.0 | all-reduce | flops 21 | bytes 168 | tf_op jit(solution)/shard_map/psum | solution.py:29
  114.3 0.1 multiply_bitcast_fusion
  114.3 132.2 %all-reduce.3.cloned.1.call-done = f32[32,80,20,20]{1,2,3,0:T(8,128)} async-done(((f32[32,80,20,20]{1,2,3,0:T(8,128)}), f32[32,80,20,20]{1,2,3,0:T(8,128)}) %all-reduce.3.cloned.1.call-update) | async-done | bytes 4096016 | tf_op jit(solution)/shard_map/psum | solution.py:29
  246.5 0.0 slice-start
  246.5 8.6 %fusion.9 = f32[8,80,32,20]{1,0,3,2:T(8,128)S(1)} fusion(f32[32,80,20,20]{1,2,3,0:T(8,128)} %all-reduce.3.cloned.1.call-done, f32[20]{0:T(128)S(1)} %get-tuple-element.4, f32[20,8]{0,1:T(8,128)S(1)} %copy-done.2), kind=kOutput, calls=%fused_computation.13 | convolution fusion | flops 99328000 | bytes 5735120 | tf_op jit(solution)/shard_map/al,vkab->lkvb/dot_general | solution.py:37
  255.2 0.0 slice-start.1
  255.2 23.4 %multiply_reduce_fusion = f32[1024,8,32]{0,2,1:T(8,128)S(1)} fusion(f32[1024,20]{0,1:T(8,128)S(1)} %multiply_bitcast_fusion, f32[8,80,32,20]{1,0,3,2:T(8,128)S(1)} %fusion.9, f32[80,8,1024,1]{2,1,0,3:T(8,128)S(1)} %bitcast.24), kind=kOutput, calls=%fused_computation | convolution fusion | flops 5043388416 | bytes 5390336 | tf_op jit(solution)/shard_map/lkvb,klc->lvbc/dot_general | solution.py:38
  278.6 1.6 copy.46
  280.2 0.0 slice-done
  280.2 0.0 slice-done.1
  280.2 1.4 multiply_reduce_fusion.1
  281.6 0.5 broadcast_multiply_fusion.3
  (2 shorter events, 0.0 us)
Async XLA Ops:
  7.2 13.4 %copy-start = (f32[80,8,1024]{2,1,0:T(8,128)S(1)}, f32[80,8,1024]{2,1,0:T(8,128)}, u32[]{:S(2)}) copy-start(f32[80,8,1024]{2,1,0:T(8,128)} %param.5) | copy-start | bytes 7864324
  7.2 239.3 %all-reduce.3.cloned.1.call-start = ((), (), s32[]{:S(2)}) async-start(), calls=%async_computation | async-start | bytes 15728640 | tf_op jit(solution)/shard_map/psum | solution.py:29
  20.6 38.6 %copy-start.2 = (f32[20,8]{0,1:T(8,128)S(1)}, f32[20,8]{0,1:T(8,128)}, u32[]{:S(2)}) copy-start(f32[20,8]{0,1:T(8,128)} %param.9) | copy-start | bytes 1924
  59.2 10.3 %copy-start.1 = (f32[20,1024]{1,0:T(8,128)S(1)}, f32[20,1024]{1,0:T(8,128)}, u32[]{:S(2)}) copy-start(f32[20,1024]{1,0:T(8,128)} %param.7) | copy-start | bytes 245764
  59.2 10.3 %copy-start.3 = (f32[1024]{0:T(1024)S(1)}, f32[1024]{0:T(1024)}, u32[]{:S(2)}) copy-start(f32[1024]{0:T(1024)} %param.8) | copy-start | bytes 12292
  246.5 33.6 %slice-start = ((s8[7864320]{0:T(1024)(128)(4,1)}), s8[4194304]{0:T(1024)(128)(4,1)S(1)}, s32[]{:S(2)}) async-start(s8[7864320]{0:T(1024)(128)(4,1)} %bitcast.25), calls=%async_computation.1 | async-start | bytes 8388608
  255.2 25.0 %slice-start.1 = ((s8[7864320]{0:T(1024)(128)(4,1)}), s8[3670016]{0:T(1024)(128)(4,1)S(1)}, s32[]{:S(2)}) async-start(s8[7864320]{0:T(1024)(128)(4,1)} %bitcast.25), calls=%async_computation.2 | async-start | bytes 7340032
Sparse Core Ops, SparseCore 0:
  69.7 176.8 all-reduce.2
where the time goes:
time: 289 us
  waiting for transfers between devices  132 us (46%)
  matrix products  80.9 us (28%)
  blocking collectives  43.9 us (15%)
  other arithmetic  15.5 us (5%)
  between operations  14.8 us (5%)
    psum x1, waiting for transfers between devices, per_device(): lax.psum((project_levels(vertical, terms), power_local, area_local), ('co...  132 us
    psum x1, blocking collectives, per_device(): lax.psum((project_levels(vertical, terms), power_local, area_local), ('co...  43.9 us
    dot_general x1, matrix products, adjoint_terms(): jnp.einsum('klc,vlbc->lkvb', perturbations, mode_products, precision=TOP_...  38.6 us
    dot_general x1, matrix products, per_device(): jnp.einsum('lkvb,klc->lvbc', lifted, perturbations, precision=TOP_PRECISION)  23.4 us
    mul x1, other arithmetic, adjoint_terms(): mode_products = weighted[:, :, None, :] * modes[None, None, :, :]  10.6 us
    dot_general x1, matrix products, project_levels(): return jnp.einsum('al,lkvb->vkab', vertical, terms, precision=TOP_PRECISION)  10.3 us
    dot_general x1, matrix products, per_device(): jnp.einsum('al,vkab->lkvb', vertical, control, precision=TOP_PRECISION)  8.63 us
  transfers between devices with their start and end apart: 1, of which 1 were waited for; matrix products, arithmetic and copies ran while one was open for 0% of the time, Pallas kernels for 0%

commit v1 on v0

v1 whole, which is shorter than its diff:
```python
import functools

import jax
import jax.numpy as jnp
from jax import lax
from jax.experimental import pallas as pl
from jax.experimental.pallas import tpu as pltpu
from jax.sharding import PartitionSpec as P

LANES = 128
NT = (((1,), (1,)), ((), ()))
TN = (((0,), (0,)), ((), ()))
NN = (((1,), (0,)), ((), ()))


def split(x):
    high = x.astype(jnp.bfloat16)
    low = (x - high.astype(jnp.float32)).astype(jnp.bfloat16)
    return high, low


def adjoint_kernel(sizes, pert_ref, grad_ref, hor_ref, area_ref, terms_ref, stat_ref):
    members, levels, vectors, modes, columns = sizes
    group = LANES // vectors
    chunks = modes // group
    used = chunks * members * levels
    if used < terms_ref.shape[0]:
        terms_ref[used:, :] = jnp.zeros((terms_ref.shape[0] - used, LANES), jnp.float32)
    area = area_ref[...]
    power = jnp.sum(area * hor_ref[...] * hor_ref[...], axis=1, keepdims=True)
    spread_power = jnp.broadcast_to(power, (modes, LANES))
    lane = lax.broadcasted_iota(jnp.int32, (modes, LANES), 1)
    row = lax.broadcasted_iota(jnp.int32, (modes, LANES), 0)
    powers = jnp.sum(jnp.where(lane == row, spread_power, 0.0), axis=0, keepdims=True)
    total = jnp.broadcast_to(jnp.sum(area, axis=1, keepdims=True), (1, LANES))
    stat_row = jnp.where(lane[:1] == modes, total, powers)
    stat_ref[...] = jnp.broadcast_to(stat_row, stat_ref.shape)

    def level(l, carry):
        high, low = split(pert_ref[:, l, :])
        both = jnp.concatenate([high, low], axis=0)
        weighted = grad_ref[:, l, :] * area
        for j in range(chunks):
            products = jnp.concatenate(
                [weighted * hor_ref[b : b + 1, :] for b in range(j * group, (j + 1) * group)],
                axis=0,
            )
            x = jnp.concatenate(split(products), axis=0)
            out = lax.dot_general(both, x, NT, preferred_element_type=jnp.float32)
            terms = out[:members, :LANES] + (out[members:, :LANES] + out[:members, LANES:])
            terms_ref[pl.ds(j * members * levels + l, members, stride=levels), :] = terms
        return carry

    for l in range(levels):
        level(l, 0)


def factor_column(stat, modes):
    lane = lax.broadcasted_iota(jnp.int32, (modes, LANES), 1)
    row = lax.broadcasted_iota(jnp.int32, (modes, LANES), 0)
    wide = jnp.broadcast_to(stat, (modes, LANES))
    power = jnp.sum(jnp.where(lane == row, wide, 0.0), axis=1, keepdims=True)
    area = jnp.sum(jnp.where(lane == modes, wide, 0.0), axis=1, keepdims=True)
    return 1.0 / jnp.sqrt(modes * (power / area + 1e-06)), area


def exchange_kernel(
    sizes, n, terms_ref, stat_ref, vert_ref, vert_t_ref, lifted_ref, parts_ref, total_ref,
    arrived, stats, reduced, verticals, weights,
    send_t, recv_t, send_s, recv_s, send_l, recv_l, send_b, recv_b, send_p, recv_p,
):
    members, levels, vectors, modes, columns = sizes
    group = LANES // vectors
    chunks = modes // group
    vmodes = vert_ref.shape[0]
    rows = terms_ref.shape[1]
    tiles = rows // levels
    me = lax.axis_index("col")
    lev = lax.axis_index("lev")
    other = 1 - lev
    mesh_id = pl.DeviceIdType.MESH
    barrier = pltpu.get_barrier_semaphore()

    def greet(p, carry):
        pl.semaphore_signal(
            barrier, inc=1, device_id=(lax.rem(me + p, n), lev), device_id_type=mesh_id
        )
        return carry

    lax.fori_loop(1, n, greet, 0)
    pl.semaphore_signal(barrier, inc=1, device_id=(me, other), device_id_type=mesh_id)
    pl.semaphore_wait(barrier, n)

    def remote(src, dst, send, recv, device):
        return pltpu.make_async_remote_copy(
            src_ref=src, dst_ref=dst, send_sem=send, recv_sem=recv,
            device_id=device, device_id_type=mesh_id,
        )

    def terms_copy(p):
        peer = lax.rem(me + p, n)
        return remote(terms_ref.at[peer], arrived.at[p], send_t.at[p], recv_t.at[p], (peer, lev))

    def stat_copy(p, slot):
        peer = lax.rem(me + p, n)
        return remote(stat_ref, stats.at[slot], send_s.at[p], recv_s.at[p], (peer, lev))

    def lifted_copy(p, slot):
        peer = lax.rem(me + p, n)
        return remote(
            lifted_ref.at[slot], lifted_ref.at[slot], send_l.at[p], recv_l.at[p], (peer, lev)
        )

    def part_copy(p, slot):
        peer = lax.rem(me + p, n)
        return remote(
            parts_ref.at[slot], parts_ref.at[slot], send_b.at[p], recv_b.at[p], (peer, lev)
        )

    def start_first(p, carry):
        stat_copy(p, me).start()
        terms_copy(p).start()
        return carry

    lax.fori_loop(1, n, start_first, 0)
    vert_copy = remote(
        vert_ref, verticals.at[lev], send_p.at[0], recv_p.at[0], (me, other)
    )
    vert_copy.start()
    stats[me] = stat_ref[...]
    verticals[lev] = vert_ref[...]
    reduced[lev] = terms_ref[me]

    def take(p, carry):
        stat_copy(p, lax.rem(me + n - p, n)).wait_recv()
        terms_copy(p).wait_recv()
        reduced[lev] += arrived[p]
        return carry

    lax.fori_loop(1, n, take, 0)
    pair_copy = remote(
        reduced.at[lev], reduced.at[lev], send_p.at[1], recv_p.at[1], (me, other)
    )
    pair_copy.start()

    def add_stat(i, carry):
        return carry + stats[i]

    stat = lax.fori_loop(0, n, add_stat, jnp.zeros(stat_ref.shape, jnp.float32))
    total_ref[...] = stat
    factor, area = factor_column(stat[:1], modes)
    factor = factor / area
    lane = lax.broadcasted_iota(jnp.int32, (modes, LANES), 1)
    row = lax.broadcasted_iota(jnp.int32, (modes, LANES), 0)
    placed = jnp.where(
        lax.div(lane, vectors) == lax.rem(row, group), jnp.broadcast_to(factor, lane.shape), 0.0
    )
    for j in range(chunks):
        weights[j : j + 1, :] = jnp.sum(
            placed[j * group : (j + 1) * group], axis=0, keepdims=True
        )
    remote(
        vert_ref, verticals.at[other], send_p.at[0], recv_p.at[0], (me, other)
    ).wait_recv()
    remote(
        reduced.at[lev], reduced.at[other], send_p.at[1], recv_p.at[1], (me, other)
    ).wait_recv()

    def wide(index):
        block = reduced[index]
        return jnp.concatenate(
            [block[i * levels : (i + 1) * levels] for i in range(tiles)], axis=1
        )

    def dot(a, b):
        return lax.dot_general(
            a, b, NN, precision=lax.Precision.HIGHEST, preferred_element_type=jnp.float32
        )

    control = dot(verticals[0][:, :levels], wide(0)) + dot(verticals[1][:, :levels], wide(1))
    lifted = dot(vert_t_ref[...][:, :vmodes], control)
    part = jnp.zeros((1, LANES), jnp.float32)
    for i in range(tiles):
        lifted_ref[me, i * levels : (i + 1) * levels, :] = lifted[:, i * LANES : (i + 1) * LANES]
        chunk = jnp.minimum(lax.div(me * tiles + i, members), chunks - 1)
        scaled = control[:, i * LANES : (i + 1) * LANES] * weights[pl.ds(chunk, 1), :]
        part = part + jnp.sum(scaled * scaled, axis=0, keepdims=True)
    parts_ref[me] = jnp.broadcast_to(part, parts_ref.shape[1:])

    def start_second(p, carry):
        lifted_copy(p, me).start()
        part_copy(p, me).start()
        return carry

    lax.fori_loop(1, n, start_second, 0)
    vert_copy.wait_send()
    pair_copy.wait_send()

    def finish(p, carry):
        source = lax.rem(me + n - p, n)
        stat_copy(p, me).wait_send()
        terms_copy(p).wait_send()
        lifted_copy(p, source).wait_recv()
        part_copy(p, source).wait_recv()
        lifted_copy(p, me).wait_send()
        part_copy(p, me).wait_send()
        return carry

    lax.fori_loop(1, n, finish, 0)


def forward_kernel(
    sizes, n, lifted_ref, parts_ref, total_ref, pert_ref, hor_ref, out_ref, bg_ref, scaled_ref
):
    members, levels, vectors, modes, columns = sizes
    group = LANES // vectors
    chunks = modes // group
    width = 256
    part = lax.fori_loop(
        0, n, lambda i, c: c + parts_ref[i], jnp.zeros(parts_ref.shape[1:], jnp.float32)
    )
    folded = part
    for g in range(1, group):
        folded = folded + pltpu.roll(part, g * vectors, 1)
    bg_ref[...] = 0.5 * folded
    factor, area = factor_column(total_ref[:1, :], modes)
    scaled_ref[...] = hor_ref[...] * (factor * (factor / area))

    def level(l, carry):
        lhs = []
        for j in range(chunks):
            high, low = split(
                lifted_ref[pl.ds(j * members * levels + l, members, stride=levels), :]
            )
            lhs.append(jnp.concatenate([high, low, high], axis=0))
        for c in range(0, columns, width):
            high, low = split(pert_ref[:, l, c : c + width])
            rhs = jnp.concatenate([high, high, low], axis=0)
            acc = None
            for j in range(chunks):
                spread = lax.dot_general(lhs[j], rhs, TN, preferred_element_type=jnp.float32)
                for g in range(group):
                    b = j * group + g
                    term = (
                        spread[g * vectors : (g + 1) * vectors]
                        * scaled_ref[b : b + 1, c : c + width]
                    )
                    acc = term if acc is None else acc + term
            out_ref[:, l, c : c + width] = acc
        return carry

    for l in range(levels):
        level(l, 0)


def per_device(perturbations, gradient, horizontal, area, vertical):
    members, levels, columns = perturbations.shape
    vectors = gradient.shape[0]
    modes = horizontal.shape[0]
    vmodes = vertical.shape[0]
    n = lax.axis_size("col")
    sizes = (members, levels, vectors, modes, columns)
    chunks = modes * vectors // LANES
    tiles = -(-chunks * members // n)
    rows = tiles * levels
    f32 = jnp.float32
    vmem = pl.BlockSpec(memory_space=pltpu.VMEM)

    terms, stat = pl.pallas_call(
        functools.partial(adjoint_kernel, sizes),
        out_shape=(
            jax.ShapeDtypeStruct((n * rows, LANES), f32),
            jax.ShapeDtypeStruct((8, LANES), f32),
        ),
        in_specs=[vmem] * 4,
        out_specs=(vmem, vmem),
        name="adjoint",
    )(perturbations, gradient, horizontal, area.reshape(1, columns))

    vert = vertical * (columns * n)
    vert_t = jnp.pad(vertical.T, ((0, 0), (0, LANES - vmodes)))
    vert = jnp.pad(vert, ((0, 0), (0, LANES - levels)))
    dma = pltpu.SemaphoreType.DMA
    lifted, parts, total = pl.pallas_call(
        functools.partial(exchange_kernel, sizes, n),
        out_shape=(
            jax.ShapeDtypeStruct((n, rows, LANES), f32),
            jax.ShapeDtypeStruct((n, 8, LANES), f32),
            jax.ShapeDtypeStruct((8, LANES), f32),
        ),
        in_specs=[vmem] * 4,
        out_specs=(vmem, vmem, vmem),
        scratch_shapes=[
            pltpu.VMEM((n, rows, LANES), f32),
            pltpu.VMEM((n, 8, LANES), f32),
            pltpu.VMEM((2, rows, LANES), f32),
            pltpu.VMEM((2, vmodes, LANES), f32),
            pltpu.VMEM((8, LANES), f32),
            dma((n,)), dma((n,)), dma((n,)), dma((n,)),
            dma((n,)), dma((n,)), dma((n,)), dma((n,)),
            dma((2,)), dma((2,)),
        ],
        compiler_params=pltpu.CompilerParams(collective_id=0, has_side_effects=True),
        name="exchange",
    )(terms.reshape(n, rows, LANES), stat, vert, vert_t)

    increment, background = pl.pallas_call(
        functools.partial(forward_kernel, sizes, n),
        out_shape=(
            jax.ShapeDtypeStruct((vectors, levels, columns), f32),
            jax.ShapeDtypeStruct((8, LANES), f32),
        ),
        in_specs=[vmem] * 5,
        out_specs=(vmem, vmem),
        scratch_shapes=[pltpu.VMEM((modes, columns), f32)],
        name="forward",
    )(lifted.reshape(n * rows, LANES), parts, total, perturbations, horizontal)
    return increment, background[0, :vectors]


def solution(mesh):
    return jax.shard_map(
        per_device,
        mesh=mesh,
        in_specs=(
            P(None, "lev", "col"),
            P(None, "lev", "col"),
            P(None, "col"),
            P("col"),
            P(None, "lev"),
        ),
        out_specs=(P(None, "lev", "col"), P()),
        check_vma=False,
    )
```

time: 289 us -> 131 us (0.45)
  the two profiles are of different devices: /device:TPU:0 before, /device:TPU:31 now
where the time goes in v1:
time: 131 us
  Pallas kernels  126 us (96%)
  local copies, waits for them, and re-layouts  3.85 us (3%)
    pallas_call x1, Pallas kernels, per_device(): pl.pallas_call(functools.partial(exchange_kernel, sizes, n), out_shape=(j...  92.7 us
    pallas_call x1, Pallas kernels, per_device(): pl.pallas_call(functools.partial(adjoint_kernel, sizes), out_shape=(jax.S...  19 us
    pallas_call x1, Pallas kernels, per_device(): pl.pallas_call(functools.partial(forward_kernel, sizes, n), out_shape=(ja...  14.7 us

profile of v1, /device:TPU:31, one launch (start us, length us, event | category | flops | bytes accessed | tf_op | source)
XLA Modules:
  0.0 130.9 jit_solution(2105917383041855576)
XLA Ops:
  0.6 1.3 pad.9.vert_t_ref
  1.9 0.8 copy.8
  2.7 0.6 pad.8.vert_ref
  3.3 19.0 %adjoint.1 = (f32[3200,128]{1,0:T(8,128)}, f32[8,128]{1,0:T(8,128)}) custom-call(f32[80,8,1024]{2,1,0:T(8,128)} %pert_ref.3, f32[32,8,1024]{2,1,0:T(8,128)} %grad_ref.1, f32[20,1024]{1,0:T(8,128)} %hor_ref.3, f32[1,1024]{1,0:T(1,128)} %bitcast.9), custom_call_target="tpu_custom_call" | custom-call | tf_op jit(solution)/shard_map/adjoint/pallas_call | solution.py:269
  22.2 92.7 %exchange.1 = (f32[16,200,128]{2,1,0:T(8,128)}, f32[16,8,128]{2,1,0:T(8,128)}, f32[8,128]{1,0:T(8,128)}) custom-call(f32[16,200,128]{2,1,0:T(8,128)} %bitcast.7, f32[8,128]{1,0:T(8,128)} %get-tuple-element.10.stat_ref, f32[20,128]{1,0:T(8,128)} %pad.8.vert_ref, f32[8,128]{1,0:T(8,128)} %pad.9.vert_t_ref), custom_call_target="tpu_custom_call" | custom-call | tf_op jit(solution)/shard_map/exchange/pallas_call | solution.py:284
  115.0 14.7 %forward.1 = (f32[32,8,1024]{2,1,0:T(8,128)}, f32[8,128]{1,0:T(8,128)}) custom-call(f32[3200,128]{1,0:T(8,128)} %bitcast.6, f32[16,8,128]{2,1,0:T(8,128)} %get-tuple-element.12.parts_ref, f32[8,128]{1,0:T(8,128)} %get-tuple-element.13.total_ref, f32[80,8,1024]{2,1,0:T(8,128)} %pert_ref.3, f32[20,1024]{1,0:T(8,128)} %hor_ref.3), custom_call_target="tpu_custom_call" | custom-call | tf_op jit(solution)/shard_map/forward/pallas_call | solution.py:307
  129.7 1.2 slice_bitcast_fusion
  (1 shorter events, 0.0 us)

commit v2 on v1

--- a/solution.py
+++ b/solution.py
@@ -66,18 +66,29 @@
 
 def exchange_kernel(
     sizes, n, terms_ref, stat_ref, vert_ref, vert_t_ref, lifted_ref, parts_ref, total_ref,
-    arrived, stats, reduced, verticals, weights,
-    send_t, recv_t, send_s, recv_s, send_l, recv_l, send_b, recv_b, send_p, recv_p,
+    first_a, first_b, second, third, stats, reduced, verticals, weights,
+    send_h, recv_h, send_g, recv_g, send_s, recv_s, send_l, recv_l, send_b, recv_b,
+    send_p, recv_p,
 ):
     members, levels, vectors, modes, columns = sizes
     group = LANES // vectors
     chunks = modes // group
     vmodes = vert_ref.shape[0]
-    rows = terms_ref.shape[1]
+    rows = terms_ref.shape[3]
     tiles = rows // levels
+    outer = n // 4
+    rows_a = first_a.shape[2]
+    half_a = pl.ds(0, rows_a)
+    half_b = pl.ds(rows_a, rows - rows_a)
     me = lax.axis_index("col")
     lev = lax.axis_index("lev")
     other = 1 - lev
+    x = lax.rem(me, 2)
+    y = lax.rem(lax.div(me, 2), 2)
+    h = lax.div(me, 4)
+    not_x, not_y = 1 - x, 1 - y
+    x_peer = (4 * h + 2 * y + not_x, lev)
+    y_peer = (4 * h + 2 * not_y + x, lev)
     mesh_id = pl.DeviceIdType.MESH
     barrier = pltpu.get_barrier_semaphore()
 
@@ -97,19 +108,23 @@
             device_id=device, device_id_type=mesh_id,
         )
 
-    def terms_copy(p):
-        peer = lax.rem(me + p, n)
-        return remote(terms_ref.at[peer], arrived.at[p], send_t.at[p], recv_t.at[p], (peer, lev))
+    def half_copy(i, src, dst, device):
+        return remote(src, dst, send_h.at[i], recv_h.at[i], device)
+
+    def outer_copy(p):
+        there = lax.rem(h + p, outer)
+        device = (4 * there + 2 * y + x, lev)
+        return remote(second.at[there], third.at[p], send_g.at[p], recv_g.at[p], device)
 
     def stat_copy(p, slot):
         peer = lax.rem(me + p, n)
         return remote(stat_ref, stats.at[slot], send_s.at[p], recv_s.at[p], (peer, lev))
 
     def lifted_copy(p, slot):
-        peer = lax.rem(me + p, n)
-        return remote(
-            lifted_ref.at[slot], lifted_ref.at[slot], send_l.at[p], recv_l.at[p], (peer, lev)
-        )
+        there = lax.rem(h + p, outer)
+        device = (4 * there + 2 * y + x, lev)
+        block = lifted_ref.at[slot, y, x]
+        return remote(block, block, send_l.at[p], recv_l.at[p], device)
 
     def part_copy(p, slot):
         peer = lax.rem(me + p, n)
@@ -117,27 +132,67 @@
             parts_ref.at[slot], parts_ref.at[slot], send_b.at[p], recv_b.at[p], (peer, lev)
         )
 
-    def start_first(p, carry):
+    one_a = half_copy(0, terms_ref.at[:, :, not_x, half_a], first_a, x_peer)
+    one_b = half_copy(1, terms_ref.at[:, not_y, :, half_b], first_b, y_peer)
+    one_a.start()
+    one_b.start()
+
+    def start_stats(p, carry):
         stat_copy(p, me).start()
-        terms_copy(p).start()
-        return carry
-
-    lax.fori_loop(1, n, start_first, 0)
+        return carry
+
+    lax.fori_loop(1, n, start_stats, 0)
     vert_copy = remote(
         vert_ref, verticals.at[lev], send_p.at[0], recv_p.at[0], (me, other)
     )
     vert_copy.start()
     stats[me] = stat_ref[...]
     verticals[lev] = vert_ref[...]
-    reduced[lev] = terms_ref[me]
+
+    def add_a(i, carry):
+        first_a[i, not_y] += terms_ref[i, not_y, x, half_a]
+        return carry
+
+    def add_b(i, carry):
+        first_b[i, not_x] += terms_ref[i, y, not_x, half_b]
+        return carry
+
+    two_a = half_copy(2, first_a.at[:, not_y], second.at[:, half_a], y_peer)
+    two_b = half_copy(3, first_b.at[:, not_x], second.at[:, half_b], x_peer)
+    one_a.wait_recv()
+    lax.fori_loop(0, outer, add_a, 0)
+    two_a.start()
+    one_b.wait_recv()
+    lax.fori_loop(0, outer, add_b, 0)
+    two_b.start()
+
+    def take_stats(p, carry):
+        stat_copy(p, lax.rem(me + n - p, n)).wait_recv()
+        return carry
+
+    lax.fori_loop(1, n, take_stats, 0)
+    two_a.wait_recv()
+    two_b.wait_recv()
+
+    def add_second(there):
+        second[there, half_a] += terms_ref[there, y, x, half_a] + first_a[there, y]
+        second[there, half_b] += terms_ref[there, y, x, half_b] + first_b[there, x]
+
+    def send_outer(p, carry):
+        add_second(lax.rem(h + p, outer))
+        outer_copy(p).start()
+        return carry
+
+    lax.fori_loop(1, outer, send_outer, 0)
+    add_second(h)
+    reduced[lev] = second[h]
 
     def take(p, carry):
-        stat_copy(p, lax.rem(me + n - p, n)).wait_recv()
-        terms_copy(p).wait_recv()
-        reduced[lev] += arrived[p]
-        return carry
-
-    lax.fori_loop(1, n, take, 0)
+        outer_copy(p).wait_recv()
+        reduced[lev] += third[p]
+        return carry
+
+    lax.fori_loop(1, outer, take, 0)
     pair_copy = remote(
         reduced.at[lev], reduced.at[lev], send_p.at[1], recv_p.at[1], (me, other)
     )
@@ -181,32 +236,61 @@
     lifted = dot(vert_t_ref[...][:, :vmodes], control)
     part = jnp.zeros((1, LANES), jnp.float32)
     for i in range(tiles):
-        lifted_ref[me, i * levels : (i + 1) * levels, :] = lifted[:, i * LANES : (i + 1) * LANES]
+        lifted_ref[h, y, x, i * levels : (i + 1) * levels, :] = lifted[:, i * LANES : (i + 1) * LANES]
         chunk = jnp.minimum(lax.div(me * tiles + i, members), chunks - 1)
         scaled = control[:, i * LANES : (i + 1) * LANES] * weights[pl.ds(chunk, 1), :]
         part = part + jnp.sum(scaled * scaled, axis=0, keepdims=True)
     parts_ref[me] = jnp.broadcast_to(part, parts_ref.shape[1:])
 
-    def start_second(p, carry):
-        lifted_copy(p, me).start()
+    def start_lifted(p, carry):
+        lifted_copy(p, h).start()
+        return carry
+
+    def start_parts(p, carry):
         part_copy(p, me).start()
         return carry
 
-    lax.fori_loop(1, n, start_second, 0)
-    vert_copy.wait_send()
-    pair_copy.wait_send()
+    def take_lifted(p, carry):
+        lifted_copy(p, lax.rem(h + outer - p, outer)).wait_recv()
+        return carry
+
+    lax.fori_loop(1, outer, start_lifted, 0)
+    lax.fori_loop(1, n, start_parts, 0)
+    lax.fori_loop(1, outer, take_lifted, 0)
+
+    def gather_copy(i, block, device):
+        return half_copy(i, block, block, device)
+
+    three_a = gather_copy(4, lifted_ref.at[:, y, x, half_a], y_peer)
+    three_b = gather_copy(5, lifted_ref.at[:, y, x, half_b], x_peer)
+    three_a.start()
+    three_b.start()
+    four_a = gather_copy(6, lifted_ref.at[:, :, x, half_a], x_peer)
+    four_b = gather_copy(7, lifted_ref.at[:, y, :, half_b], y_peer)
+    gather_copy(4, lifted_ref.at[:, not_y, x, half_a], y_peer).wait_recv()
+    four_a.start()
+    gather_copy(5, lifted_ref.at[:, y, not_x, half_b], x_peer).wait_recv()
+    four_b.start()
+    for copy in (one_a, one_b, two_a, two_b, three_a, three_b, vert_copy, pair_copy):
+        copy.wait_send()
 
     def finish(p, carry):
-        source = lax.rem(me + n - p, n)
         stat_copy(p, me).wait_send()
-        terms_copy(p).wait_send()
-        lifted_copy(p, source).wait_recv()
-        part_copy(p, source).wait_recv()
-        lifted_copy(p, me).wait_send()
+        part_copy(p, lax.rem(me + n - p, n)).wait_recv()
         part_copy(p, me).wait_send()
         return carry
 
+    def finish_outer(p, carry):
+        outer_copy(p).wait_send()
+        lifted_copy(p, h).wait_send()
+        return carry
+
     lax.fori_loop(1, n, finish, 0)
+    lax.fori_loop(1, outer, finish_outer, 0)
+    gather_copy(6, lifted_ref.at[:, :, not_x, half_a], x_peer).wait_recv()
+    gather_copy(7, lifted_ref.at[:, not_y, :, half_b], y_peer).wait_recv()
+    four_a.wait_send()
+    four_b.wait_send()
 
 
 def forward_kernel(
@@ -263,6 +347,8 @@
     chunks = modes * vectors // LANES
     tiles = -(-chunks * members // n)
     rows = tiles * levels
+    outer = n // 4
+    rows_a = (tiles + 1) // 2 * levels
     f32 = jnp.float32
     vmem = pl.BlockSpec(memory_space=pltpu.VMEM)
 
@@ -284,25 +370,28 @@
     lifted, parts, total = pl.pallas_call(
         functools.partial(exchange_kernel, sizes, n),
         out_shape=(
-            jax.ShapeDtypeStruct((n, rows, LANES), f32),
+            jax.ShapeDtypeStruct((outer, 2, 2, rows, LANES), f32),
             jax.ShapeDtypeStruct((n, 8, LANES), f32),
             jax.ShapeDtypeStruct((8, LANES), f32),
         ),
         in_specs=[vmem] * 4,
         out_specs=(vmem, vmem, vmem),
         scratch_shapes=[
-            pltpu.VMEM((n, rows, LANES), f32),
+            pltpu.VMEM((outer, 2, rows_a, LANES), f32),
+            pltpu.VMEM((outer, 2, rows - rows_a, LANES), f32),
+            pltpu.VMEM((outer, rows, LANES), f32),
+            pltpu.VMEM((outer, rows, LANES), f32),
             pltpu.VMEM((n, 8, LANES), f32),
             pltpu.VMEM((2, rows, LANES), f32),
             pltpu.VMEM((2, vmodes, LANES), f32),
             pltpu.VMEM((8, LANES), f32),
-            dma((n,)), dma((n,)), dma((n,)), dma((n,)),
-            dma((n,)), dma((n,)), dma((n,)), dma((n,)),
+            dma((8,)), dma((8,)), dma((outer,)), dma((outer,)), dma((n,)), dma((n,)),
+            dma((outer,)), dma((outer,)), dma((n,)), dma((n,)),
             dma((2,)), dma((2,)),
         ],
         compiler_params=pltpu.CompilerParams(collective_id=0, has_side_effects=True),
         name="exchange",
-    )(terms.reshape(n, rows, LANES), stat, vert, vert_t)
+    )(terms.reshape(outer, 2, 2, rows, LANES), stat, vert, vert_t)
 
     increment, background = pl.pallas_call(
         functools.partial(forward_kernel, sizes, n),

time: 131 us -> 102 us (0.78)
  the two profiles are of different devices: /device:TPU:31 before, /device:TPU:0 now
where the time goes in v2:
time: 102 us
  Pallas kernels  97.7 us (96%)
  local copies, waits for them, and re-layouts  3.85 us (4%)
    pallas_call x1, Pallas kernels, per_device(): pl.pallas_call(functools.partial(exchange_kernel, sizes, n), out_shape=(j...  64.1 us
    pallas_call x1, Pallas kernels, per_device(): pl.pallas_call(functools.partial(adjoint_kernel, sizes), out_shape=(jax.S...  19 us
    pallas_call x1, Pallas kernels, per_device(): pl.pallas_call(functools.partial(forward_kernel, sizes, n), out_shape=(ja...  14.7 us

profile of v2, /device:TPU:0, one launch (start us, length us, event | category | flops | bytes accessed | tf_op | source)
XLA Modules:
  0.0 102.2 jit_solution(1713238321363608829)
XLA Ops:
  0.6 1.3 %pad.9.vert_t_ref = f32[8,128]{1,0:T(8,128)} pad(f32[8,20]{1,0:T(8,128)} %bitcast.8, f32[]{:T(128)} %constant.4.clone.1), padding=0_0x0_108 | pad | bytes 4740 | tf_op jit(solution)/shard_map/jit(_pad)/pad | solution.py:367
  1.9 0.8 copy.8
  2.7 0.6 pad.8.vert_ref
  3.3 19.0 %adjoint.1 = (f32[3200,128]{1,0:T(8,128)}, f32[8,128]{1,0:T(8,128)}) custom-call(f32[80,8,1024]{2,1,0:T(8,128)} %pert_ref.3, f32[32,8,1024]{2,1,0:T(8,128)} %grad_ref.1, f32[20,1024]{1,0:T(8,128)} %hor_ref.3, f32[1,1024]{1,0:T(1,128)} %bitcast.9), custom_call_target="tpu_custom_call" | custom-call | tf_op jit(solution)/shard_map/adjoint/pallas_call | solution.py:355
  22.3 64.1 %exchange.1 = (f32[4,2,2,200,128]{4,3,2,1,0:T(8,128)}, f32[16,8,128]{2,1,0:T(8,128)}, f32[8,128]{1,0:T(8,128)}) custom-call(f32[4,2,2,200,128]{4,3,2,1,0:T(8,128)} %bitcast.7, f32[8,128]{1,0:T(8,128)} %get-tuple-element.10.stat_ref, f32[20,128]{1,0:T(8,128)} %pad.8.vert_ref, f32[8,128]{1,0:T(8,128)} %pad.9.vert_t_ref), custom_call_target="tpu_custom_call" | custom-call | tf_op jit(solution)/shard_map/exchange/pallas_call | solution.py:370
  86.3 14.7 %forward.1 = (f32[32,8,1024]{2,1,0:T(8,128)}, f32[8,128]{1,0:T(8,128)}) custom-call(f32[3200,128]{1,0:T(8,128)} %bitcast.6, f32[16,8,128]{2,1,0:T(8,128)} %get-tuple-element.12.parts_ref, f32[8,128]{1,0:T(8,128)} %get-tuple-element.13.total_ref, f32[80,8,1024]{2,1,0:T(8,128)} %pert_ref.3, f32[20,1024]{1,0:T(8,128)} %hor_ref.3), custom_call_target="tpu_custom_call" | custom-call | tf_op jit(solution)/shard_map/forward/pallas_call | solution.py:396
  101.0 1.2 %slice_bitcast_fusion = f32[32]{0:T(128)} fusion(f32[8,128]{1,0:T(8,128)} %get-tuple-element.15), kind=kLoop, calls=%fused_computation.1 | loop fusion | bytes 256 | tf_op jit(solution)/shard_map/squeeze | solution.py:407
  (1 shorter events, 0.0 us)

commit v3 on v2

--- a/solution.py
+++ b/solution.py
@@ -233,7 +233,10 @@
         )
 
     control = dot(verticals[0][:, :levels], wide(0)) + dot(verticals[1][:, :levels], wide(1))
-    lifted = dot(vert_t_ref[...][:, :vmodes], control)
+    lifted = lax.dot_general(
+        vert_t_ref[...], control, TN, precision=lax.Precision.HIGHEST,
+        preferred_element_type=jnp.float32,
+    )
     part = jnp.zeros((1, LANES), jnp.float32)
     for i in range(tiles):
         lifted_ref[h, y, x, i * levels : (i + 1) * levels, :] = lifted[:, i * LANES : (i + 1) * LANES]
@@ -364,7 +367,6 @@
     )(perturbations, gradient, horizontal, area.reshape(1, columns))
 
     vert = vertical * (columns * n)
-    vert_t = jnp.pad(vertical.T, ((0, 0), (0, LANES - vmodes)))
     vert = jnp.pad(vert, ((0, 0), (0, LANES - levels)))
     dma = pltpu.SemaphoreType.DMA
     lifted, parts, total = pl.pallas_call(
@@ -391,7 +393,7 @@
         ],
         compiler_params=pltpu.CompilerParams(collective_id=0, has_side_effects=True),
         name="exchange",
-    )(terms.reshape(outer, 2, 2, rows, LANES), stat, vert, vert_t)
+    )(terms.reshape(outer, 2, 2, rows, LANES), stat, vert, vertical)
 
     increment, background = pl.pallas_call(
         functools.partial(forward_kernel, sizes, n),

time: 102 us -> 101 us (level)
  local copies, waits for them, and re-layouts: 3.85 us -> 2.57 us
    pad x1 -> x0, local copies, waits for them, and re-layouts: 1.28 us -> none  [per_device(): vert_t = jnp.pad(vertical.T, ((0, 0), (0, LANES - vmodes)))]
where the time goes in v3:
time: 101 us
  Pallas kernels  97.6 us (97%)
  local copies, waits for them, and re-layouts  2.57 us (3%)
    pallas_call x1, Pallas kernels, per_device(): pl.pallas_call(functools.partial(exchange_kernel, sizes, n), out_shape=(j...  64 us
    pallas_call x1, Pallas kernels, per_device(): pl.pallas_call(functools.partial(adjoint_kernel, sizes), out_shape=(jax.S...  18.9 us
    pallas_call x1, Pallas kernels, per_device(): pl.pallas_call(functools.partial(forward_kernel, sizes, n), out_shape=(ja...  14.7 us

profile of v3, /device:TPU:0, one launch (start us, length us, event | category | flops | bytes accessed | tf_op | source)
XLA Modules:
  0.0 100.9 jit_solution(6055029143644696025)
XLA Ops:
  0.6 0.8 copy.9.vert_t_ref
  1.4 0.0 copy-start
  1.4 0.6 pad.4.vert_ref
  2.0 18.9 %adjoint.1 = (f32[3200,128]{1,0:T(8,128)}, f32[8,128]{1,0:T(8,128)}) custom-call(f32[80,8,1024]{2,1,0:T(8,128)} %pert_ref.3, f32[32,8,1024]{2,1,0:T(8,128)} %grad_ref.1, f32[20,1024]{1,0:T(8,128)} %hor_ref.3, f32[1,1024]{1,0:T(1,128)} %bitcast.7), custom_call_target="tpu_custom_call" | custom-call | tf_op jit(solution)/shard_map/adjoint/pallas_call | solution.py:358
  21.0 0.0 copy-done
  21.0 64.0 %exchange.1 = (f32[4,2,2,200,128]{4,3,2,1,0:T(8,128)}, f32[16,8,128]{2,1,0:T(8,128)}, f32[8,128]{1,0:T(8,128)}) custom-call(f32[4,2,2,200,128]{4,3,2,1,0:T(8,128)} %bitcast.6, f32[8,128]{1,0:T(8,128)} %get-tuple-element.10.stat_ref, f32[20,128]{1,0:T(8,128)} %pad.4.vert_ref, f32[20,8]{1,0:T(8,128)} %copy-done), custom_call_target="tpu_custom_call" | custom-call | tf_op jit(solution)/shard_map/exchange/pallas_call | solution.py:372
  85.0 14.7 %forward.1 = (f32[32,8,1024]{2,1,0:T(8,128)}, f32[8,128]{1,0:T(8,128)}) custom-call(f32[3200,128]{1,0:T(8,128)} %bitcast.5, f32[16,8,128]{2,1,0:T(8,128)} %get-tuple-element.12.parts_ref, f32[8,128]{1,0:T(8,128)} %get-tuple-element.13.total_ref, f32[80,8,1024]{2,1,0:T(8,128)} %pert_ref.3, f32[20,1024]{1,0:T(8,128)} %hor_ref.3), custom_call_target="tpu_custom_call" | custom-call | tf_op jit(solution)/shard_map/forward/pallas_call | solution.py:398
  99.7 1.2 %slice_bitcast_fusion = f32[32]{0:T(128)} fusion(f32[8,128]{1,0:T(8,128)} %get-tuple-element.15), kind=kLoop, calls=%fused_computation.1 | loop fusion | bytes 256 | tf_op jit(solution)/shard_map/squeeze | solution.py:409
  (1 shorter events, 0.0 us)
Async XLA Ops:
  1.4 19.6 %copy-start = (f32[20,8]{1,0:T(8,128)}, f32[20,8]{1,0:T(8,128)S(1)}, u32[]{:S(2)}) copy-start(f32[20,8]{1,0:T(8,128)S(1)} %copy.9.vert_t_ref) | copy-start | bytes 1924
